TPU v7x, 32 devices: a whole 2x2x4 slice. The times are simulated.
32 devices in a mesh: fsdp: 16 (over z, x, core), tp: 2 (over y).
Axes of the slice: x: 2, y: 2, z: 4, core: 2. Of those that a mesh axis runs over, the one named last changes fastest.
Arguments:
- hidden: bfloat16 [4096, 8192], P('fsdp'), may hold values from -6 to 6
- norm_gain: float32 [8192], replicated, may hold values from 0.6 to 6, as said below
- w_query: bfloat16 [8192, 4096], P('fsdp', 'tp'), may hold values from -0.09375 to 0.09375
- w_key: bfloat16 [8192, 512], P('fsdp'), may hold values from -0.09375 to 0.09375
- w_value: bfloat16 [8192, 512], P('fsdp'), may hold values from -0.0625 to 0.0625
- bias_query: bfloat16 [4096], P('tp'), may hold values from -3 to 3
- bias_key: bfloat16 [512], replicated, may hold values from -3 to 3
- bias_value: bfloat16 [512], replicated, may hold values from -3 to 3
- w_out: bfloat16 [4096, 8192], P('tp', 'fsdp'), may hold values from -0.09375 to 0.09375
- seq_lengths: int32 [4], replicated, may hold values from 1 to 3072, 4096 in all
Outputs:
- hidden_out: float32 [4096, 8192], P(('fsdp', 'tp'))
Inputs may be any that keep to these rules, and one draw needn't show every extreme that they name: `seq_lengths`: 4 sequences packed in order; the lengths sum to 4096 and the longest has exactly 3072 tokens. `norm_gain`: positive gains.
All inputs are finite; a program needn't handle non-finite values.
Results may differ from a plain program's by a relative error of at most 0.014.
The roundings to bfloat16 on the way count: a program that leaves them out, or rounds other values in their place, can miss the bound.
Values may be sent and summed in bfloat16 or wider, within the bound.
A program may use at most 128 MiB of HBM per device.

v0:
```python
import math
import jax
import jax.numpy as jnp
from jax import lax
from jax.sharding import PartitionSpec as P

HEAD = 128
QHEADS = 32
KVHEADS = 4
ROPE_BASE = 1000000.0
EPSILON = 1e-06
FLOOR = -1e30


def token_layout(seq_lengths, token_index):
    seq_ends = jnp.cumsum(seq_lengths)
    seq_starts = seq_ends - seq_lengths
    member = (token_index[:, None] >= seq_ends[None, :]).astype(jnp.int32)
    segment = jnp.sum(member, axis=1)
    one_hot = segment[:, None] == jnp.arange(seq_lengths.shape[0], dtype=jnp.int32)[None, :]
    seq_begin = jnp.sum(jnp.where(one_hot, seq_starts[None, :], 0), axis=1)
    return (segment, token_index - seq_begin)


def rotary(vectors, position):
    half_size = vectors.shape[-1] // 2
    frequency = jnp.exp(
        jnp.arange(half_size, dtype=jnp.float32) * (-2.0 * math.log(ROPE_BASE) / vectors.shape[-1])
    )
    angle = position.astype(jnp.float32)[:, None] * frequency[None, :]
    cos_table = jnp.concatenate([jnp.cos(angle), jnp.cos(angle)], axis=1)[:, None, :]
    sin_table = jnp.concatenate([jnp.sin(angle), jnp.sin(angle)], axis=1)[:, None, :]
    turned = jnp.concatenate([-vectors[..., half_size:], vectors[..., :half_size]], axis=-1)
    return vectors * cos_table + turned * sin_table


def shards(
    hidden, norm_gain, w_query, w_key, w_value, bias_query, bias_key, bias_value, w_out, seq_lengths
):
    tok_rows = hidden.shape[0]
    first_row = lax.axis_index("fsdp") * tok_rows
    local_index = first_row + jnp.arange(tok_rows, dtype=jnp.int32)
    segment, position = token_layout(seq_lengths, local_index)
    widened = hidden.astype(jnp.float32)
    scale = lax.rsqrt(jnp.mean(widened * widened, axis=1, keepdims=True) + EPSILON)
    normed = (widened * scale * norm_gain[None, :]).astype(jnp.bfloat16)
    query_cols = w_query.shape[1]
    local_heads = query_cols // HEAD
    group_size = QHEADS // KVHEADS
    local_kv = max(local_heads // group_size, 1)
    first_kv = lax.axis_index("tp") * local_heads // group_size
    key_cols = local_kv * HEAD
    key_part = lax.dynamic_slice_in_dim(w_key, first_kv * HEAD, key_cols, 1)
    value_part = lax.dynamic_slice_in_dim(w_value, first_kv * HEAD, key_cols, 1)
    key_bias = lax.dynamic_slice_in_dim(bias_key, first_kv * HEAD, key_cols, 0)
    value_bias = lax.dynamic_slice_in_dim(bias_value, first_kv * HEAD, key_cols, 0)
    pieces = (
        lax.all_gather(w_query, "fsdp", axis=0, tiled=True),
        lax.all_gather(key_part, "fsdp", axis=0, tiled=True),
        lax.all_gather(value_part, "fsdp", axis=0, tiled=True),
    )
    query, keys, values = tuple(
        (jnp.dot(normed, piece, preferred_element_type=jnp.float32) for piece in pieces)
    )
    query = rotary(
        (query + bias_query.astype(jnp.float32)[None, :]).reshape(tok_rows, -1, HEAD), position
    ).astype(jnp.bfloat16)
    keys = rotary(
        (keys + key_bias.astype(jnp.float32)[None, :]).reshape(tok_rows, -1, HEAD), position
    ).astype(jnp.bfloat16)
    values = (values + value_bias.astype(jnp.float32)[None, :]).astype(jnp.bfloat16)
    keys = keys.reshape(tok_rows, key_cols)
    per_kv = local_heads // local_kv
    query_grid = query.reshape(tok_rows, local_kv, per_kv, HEAD)
    start_state = (
        jnp.full((local_kv, per_kv, tok_rows), FLOOR, jnp.float32),
        jnp.zeros((local_kv, per_kv, tok_rows), jnp.float32),
        jnp.zeros((local_kv, per_kv, tok_rows, HEAD), jnp.float32),
    )
    key_piece = lax.all_gather(keys, "fsdp", axis=0, tiled=True)
    value_piece = lax.all_gather(values, "fsdp", axis=0, tiled=True)
    piece_rows = key_piece.shape[0]
    shard_count = max(piece_rows // tok_rows, 1)
    per_block = 1
    for divisor in range(1, 9):
        if shard_count % divisor == 0:
            per_block = divisor
    block_rows = min(per_block * tok_rows, piece_rows)
    block_count = piece_rows // block_rows

    def fold_block(block_number, carried):
        running_max, total, accumulated = carried
        offset = block_number * block_rows
        key_block = lax.dynamic_slice_in_dim(key_piece, offset, block_rows, 0).reshape(
            block_rows, local_kv, HEAD
        )
        value_block = lax.dynamic_slice_in_dim(value_piece, offset, block_rows, 0).reshape(
            block_rows, local_kv, HEAD
        )
        key_index = offset + jnp.arange(block_rows, dtype=jnp.int32)
        key_segment, unused = token_layout(seq_lengths, key_index)
        scores = jnp.einsum(
            "qkgd,nkd->kgqn", query_grid, key_block, preferred_element_type=jnp.float32
        ) * HEAD ** (-0.5)
        allowed = (
            (segment[:, None] == key_segment[None, :])
            & (local_index[:, None] >= key_index[None, :])
        )[None, None]
        scores = jnp.where(allowed, scores, FLOOR)
        new_max = jnp.maximum(running_max, jnp.max(scores, axis=3))
        weights = jnp.where(allowed, jnp.exp(scores - new_max[..., None]), 0.0)
        factor = jnp.exp(running_max - new_max)
        total = total * factor + jnp.sum(weights, axis=3)
        update = jnp.einsum(
            "kgqn,nkd->kgqd",
            weights.astype(jnp.bfloat16),
            value_block,
            preferred_element_type=jnp.float32,
        )
        accumulated = accumulated * factor[..., None] + update
        return (new_max, total, accumulated)

    final_state = lax.fori_loop(0, block_count, fold_block, start_state)
    mixed = final_state[2] / final_state[1][..., None]
    attended = jnp.transpose(mixed, (2, 0, 1, 3)).reshape(tok_rows, query_cols).astype(jnp.bfloat16)
    share_rows = tok_rows // lax.axis_size("tp")
    own_rows = lax.dynamic_slice_in_dim(
        hidden, lax.axis_index("tp") * share_rows, share_rows, 0
    ).astype(jnp.float32)
    terms = jnp.dot(
        attended,
        lax.all_gather(w_out, "fsdp", axis=1, tiled=True),
        preferred_element_type=jnp.float32,
    )
    summed = lax.psum_scatter(
        terms.astype(jnp.bfloat16), "tp", scatter_dimension=0, tiled=True
    ).astype(jnp.float32)
    return own_rows + summed


def solution(mesh):
    in_specs = (
        P("fsdp", None),
        P(),
        P("fsdp", "tp"),
        P("fsdp", None),
        P("fsdp", None),
        P("tp"),
        P(),
        P(),
        P("tp", "fsdp"),
        P(),
    )
    out_specs = P(("fsdp", "tp"), None)
    return jax.shard_map(shards, mesh=mesh, in_specs=in_specs, out_specs=out_specs, check_vma=False)
```

profile of v0, /device:TPU:0, one launch (start us, length us, event | category | flops | bytes accessed | tf_op | source)
XLA Modules:
  0.0 618.8 jit_solution(51648293795599105)
XLA Ops:
  6.5 1.0 copy-done
  7.6 0.7 constant_dynamic-slice_fusion.3
  8.4 1.7 constant_dynamic-slice_fusion.2
  10.2 0.7 all-gather.11.cloned.1.call-update
  10.9 0.8 reduce-window.9
  11.9 0.7 bitcast_subtract_fusion
  12.6 0.5 multiply_cosine_fusion
  13.2 0.1 pad_maximum_fusion.1
  13.7 3.1 fusion.15
  16.8 45.9 %all-gather.7.cloned.1.call-done = bf16[8192,256]{1,0:T(8,128)(2,1)} async-done(((bf16[512,256]{1,0:T(8,128)(2,1)}), bf16[8192,256]{1,0:T(8,128)(2,1)}) %all-gather.7.cloned.1.call-update) | async-done | bytes 4194320 | tf_op jit(solution)/shard_map/all_gather | solution.py:59
  62.7 5.6 convolution_add_fusion.2
  68.3 0.7 fusion.21
  69.2 44.6 %all-gather.13.cloned.1.call-done = bf16[8192,256]{1,0:T(8,128)(2,1)} async-done(((bf16[512,256]{1,0:T(8,128)(2,1)}), bf16[8192,256]{1,0:T(8,128)(2,1)}) %all-gather.13.cloned.1.call-update) | async-done | bytes 4194320 | tf_op jit(solution)/shard_map/all_gather | solution.py:60
  113.8 5.4 fusion.20
  119.3 0.5 all-gather.17.cloned.1.call-update
  119.8 0.2 reduce-scatter.2.cloned.1.call-start
  120.1 0.2 broadcast_in_dim.117
  120.3 161.7 %all-gather.11.cloned.1.call-done = bf16[8192,2048]{1,0:T(8,128)(2,1)} async-done(((bf16[512,2048]{1,0:T(8,128)(2,1)}), bf16[8192,2048]{1,0:T(8,128)(2,1)}) %all-gather.11.cloned.1.call-update) | async-done | bytes 33554448 | tf_op jit(solution)/shard_map/all_gather | solution.py:58
  282.0 16.5 %convolution_add_fusion = f32[256,2048]{1,0:T(8,128)S(1)} fusion(bf16[8192,2048]{1,0:T(8,128)(2,1)} %all-gather.11.cloned.1.call-done, f32[2048]{0:T(1024)S(1)} %convert_element_type.80, bf16[256,8192]{1,0:T(8,128)(2,1)} %param.12, f32[8192]{0:T(1024)S(1)} %copy-done.8, f32[256]{0:T(256)S(1)} %add_rsqrt_fusion), kind=kOutput, calls=%fused_computation.30 | convolution fusion | flops 8598847488 | bytes 39887872 | tf_op jit(solution)/shard_map/dot_general | solution.py:63
  298.5 1.9 copy.44
  300.3 3.1 slice_negate_fusion
  303.5 3.2 copy.45
  306.6 3.2 copy.46
  309.9 0.4 copy.57
  310.2 1.2 copy-done.3
  311.4 0.6 copy-done.4
  312.1 1.0 fusion.19
  313.1 12.0 %all-gather.9.cloned.1.call-done = bf16[4096,256]{0,1:T(8,128)(2,1)} async-done(((bf16[256,256]{0,1:T(8,128)(2,1)}), bf16[4096,256]{0,1:T(8,128)(2,1)}) %all-gather.9.cloned.1.call-update) | async-done | bytes 2097168 | tf_op jit(solution)/shard_map/all_gather | solution.py:80
  325.1 42.6 %all-gather.15.cloned.1.call-done = bf16[4096,256]{1,0:T(8,128)(2,1)} async-done(((bf16[256,256]{1,0:T(8,128)(2,1)}), bf16[4096,256]{1,0:T(8,128)(2,1)}) %all-gather.15.cloned.1.call-update) | async-done | bytes 2097168 | tf_op jit(solution)/shard_map/all_gather | solution.py:81
  367.6 104.9 %while.20 = (s32[]{:T(128)}, f32[2,8,256]{2,1,0:T(8,128)S(1)}, f32[2,8,256]{2,1,0:T(8,128)S(1)}, f32[2,8,256,128]{3,2,1,0:T(8,128)}, s32[256]{0:T(256)S(1)}, /*i...) while((s32[]{:T(128)}, f32[2,8,256]{2,1,0:T(8,128)S(1)}, ...), condition=%wide.region_9.10_spmd.clone, body=%wide.region_5.9_spmd.clone.sunk | while | flops 4407209984 | bytes 125086968 | solution.py:123
  367.6 1.3 constant_dynamic-slice_fusion.6
  369.1 1.4 compare_and_fusion.2
  370.5 15.2 %fusion.45 = (f32[2,8,256]{2,1,0:T(8,128)S(1)}, f32[2,2048,256,8]{2,1,3,0:T(8,128)}) fusion(pred[256,2048]{0,1:T(8,128)(4,1)S(1)} %compare_and_fusion.2, bf16[2048,2,128,1]{0,2,3,1:T(8,128)(2,1)S(1)} %bitcast.72, bf16[256,2,8,128]{3,0,2,1:T(8,128)(2,1)S(1)} %get-tuple-element.451), kind=kOutput, calls=%fused_computation.3.clone.1 | convolution fusion | flops 2172645376 | bytes 36192256 | tf_op jit(solution)/shard_map/while/body/eval_jaxpr/qkgd,nkd->kgqn/dot_general | solution.py:102
  385.7 15.3 %fusion.46 = f32[2,8,256]{2,1,0:T(8,128)S(1)} fusion(f32[2,2048,256,8]{2,1,3,0:T(8,128)} %get-tuple-element.413, f32[2,8,256]{2,1,0:T(8,128)S(1)} %select_maximum_fusion.2, pred[256,2048]{0,1:T(8,128)(4,1)S(1)} %compare_and_fusion.2), kind=kLoop, calls=%fused_computation.5.clone.1 | loop fusion | flops 41938944 | bytes 34111488 | tf_op jit(solution)/shard_map/while/body/eval_jaxpr/reduce_sum | solution.py:113
  401.2 1.4 copy.62
  402.6 17.6 %fusion.48 = f32[2,8,256,128]{3,2,1,0:T(8,128)} fusion(f32[2,8,256,128]{3,2,1,0:T(8,128)} %get-tuple-element.433, bf16[2048,2,128,1]{0,2,3,1:T(8,128)(2,1)} %bitcast.73, f32[2,2048,256,8]{2,1,3,0:T(8,128)} %get-tuple-element.413, f32[2,8,256]{2,1,0:T(8,128)S(1)} %select_maximum_fusion.2, pred[256,2048]{0,1:T(8,128)(4,1)S(1)} %compare_and_fusion.2, ...), kind=kOutput, calls=%fused_computation.9.clone.1 | convolution fusion | flops 2190999552 | bytes 39354368 | tf_op jit(solution)/shard_map/while/body/eval_jaxpr/kgqn,nkd->kgqd/dot_general | solution.py:114
  420.2 1.3 constant_dynamic-slice_fusion.6
  421.7 1.4 compare_and_fusion.2
  423.1 14.1 %fusion.45 = (f32[2,8,256]{2,1,0:T(8,128)S(1)}, f32[2,2048,256,8]{2,1,3,0:T(8,128)}) fusion(pred[256,2048]{0,1:T(8,128)(4,1)S(1)} %compare_and_fusion.2, bf16[2048,2,128,1]{0,2,3,1:T(8,128)(2,1)S(1)} %bitcast.72, bf16[256,2,8,128]{3,0,2,1:T(8,128)(2,1)S(1)} %get-tuple-element.451), kind=kOutput, calls=%fused_computation.3.clone.1 | convolution fusion | flops 2172645376 | bytes 36192256 | tf_op jit(solution)/shard_map/while/body/eval_jaxpr/qkgd,nkd->kgqn/dot_general | solution.py:102
  437.3 15.6 %fusion.46 = f32[2,8,256]{2,1,0:T(8,128)S(1)} fusion(f32[2,2048,256,8]{2,1,3,0:T(8,128)} %get-tuple-element.413, f32[2,8,256]{2,1,0:T(8,128)S(1)} %select_maximum_fusion.2, pred[256,2048]{0,1:T(8,128)(4,1)S(1)} %compare_and_fusion.2), kind=kLoop, calls=%fused_computation.5.clone.1 | loop fusion | flops 41938944 | bytes 34111488 | tf_op jit(solution)/shard_map/while/body/eval_jaxpr/reduce_sum | solution.py:113
  452.9 1.4 copy.62
  454.4 18.2 %fusion.48 = f32[2,8,256,128]{3,2,1,0:T(8,128)} fusion(f32[2,8,256,128]{3,2,1,0:T(8,128)} %get-tuple-element.433, bf16[2048,2,128,1]{0,2,3,1:T(8,128)(2,1)} %bitcast.73, f32[2,2048,256,8]{2,1,3,0:T(8,128)} %get-tuple-element.413, f32[2,8,256]{2,1,0:T(8,128)S(1)} %select_maximum_fusion.2, pred[256,2048]{0,1:T(8,128)(4,1)S(1)} %compare_and_fusion.2, ...), kind=kOutput, calls=%fused_computation.9.clone.1 | convolution fusion | flops 2190999552 | bytes 39354368 | tf_op jit(solution)/shard_map/while/body/eval_jaxpr/kgqn,nkd->kgqd/dot_general | solution.py:114
  472.6 2.1 copy.48
  474.7 1.2 divide_convert_fusion
  475.9 59.9 %all-gather.17.cloned.1.call-done = bf16[2048,8192]{1,0:T(8,128)(2,1)} async-done(((bf16[2048,512]{1,0:T(8,128)(2,1)}), bf16[2048,8192]{1,0:T(8,128)(2,1)}) %all-gather.17.cloned.1.call-update) | async-done | bytes 33554448 | tf_op jit(solution)/shard_map/all_gather | solution.py:132
  535.9 16.8 %convolution_convert_fusion = bf16[256,8192]{1,0:T(8,128)(2,1)} fusion(bf16[256,2048]{0,1:T(8,128)(2,1)} %bitcast.77, bf16[2048,8192]{1,0:T(8,128)(2,1)} %all-gather.17.cloned.1.call-done), kind=kOutput, calls=%fused_computation.25 | convolution fusion | flops 8592031744 | bytes 38797312 | tf_op jit(solution)/shard_map/dot_general | solution.py:130
  552.7 54.5 %reduce-scatter.2.cloned.1.call-done = bf16[128,8192]{1,0:T(8,128)(2,1)} async-done(((bf16[256,8192]{1,0:T(8,128)(2,1)}), bf16[128,8192]{1,0:T(8,128)(2,1)}) %reduce-scatter.2.cloned.1.call-update) | async-done | bytes 2097168 | tf_op jit(solution)/shard_map/reduce_scatter | solution.py:135
  607.2 4.8 convert_add_fusion
  (61 shorter events, 1.4 us)
Async XLA Ops:
  6.5 1.0 copy-start
  6.5 7.0 %copy-start.6 = (bf16[512]{0:T(512)(128)(2,1)S(1)}, bf16[512]{0:T(512)(128)(2,1)}, u32[]{:S(2)}) copy-start(bf16[512]{0:T(512)(128)(2,1)} %param.18) | copy-start | bytes 3076
  6.5 56.1 %all-gather.7.cloned.1.call-start = ((), (), s32[]{:S(2)}) async-start(), calls=%async_computation.1 | async-start | bytes 4456448 | tf_op jit(solution)/shard_map/all_gather | solution.py:59
  8.3 54.4 %copy-start.8 = (f32[8192]{0:T(1024)S(1)}, f32[8192]{0:T(1024)}, u32[]{:S(2)}) copy-start(f32[8192]{0:T(1024)} %param.13) | copy-start | bytes 98308
  8.3 105.4 %all-gather.13.cloned.1.call-start = ((), (), s32[]{:S(2)}) async-start(), calls=%async_computation.4 | async-start | bytes 4456448 | tf_op jit(solution)/shard_map/all_gather | solution.py:60
  10.1 271.9 %all-gather.11.cloned.1.call-start = ((), (), s32[]{:S(2)}) async-start(), calls=%async_computation.3 | async-start | bytes 35651584 | tf_op jit(solution)/shard_map/all_gather | solution.py:58
  10.9 314.2 %all-gather.9.cloned.1.call-start = ((), (), s32[]{:S(2)}) async-start(), calls=%async_computation.2 | async-start | bytes 2228224 | tf_op jit(solution)/shard_map/all_gather | solution.py:80
  16.8 52.3 %copy-start.7 = (bf16[512]{0:T(512)(128)(2,1)S(1)}, bf16[512]{0:T(512)(128)(2,1)}, u32[]{:S(2)}) copy-start(bf16[512]{0:T(512)(128)(2,1)} %param.19) | copy-start | bytes 3076
  69.0 298.6 %all-gather.15.cloned.1.call-start = ((), (), s32[]{:S(2)}) async-start(), calls=%async_computation.5 | async-start | bytes 2228224 | tf_op jit(solution)/shard_map/all_gather | solution.py:81
  69.2 50.9 %copy-start.5 = (bf16[2048]{0:T(1024)(128)(2,1)S(1)}, bf16[2048]{0:T(1024)(128)(2,1)}, u32[]{:S(2)}) copy-start(bf16[2048]{0:T(1024)(128)(2,1)} %param.17) | copy-start | bytes 12292
  69.2 50.9 %copy-start.9 = (s32[4]{0:T(128)S(1)}, s32[4]{0:T(128)}, u32[]{:S(2)}) copy-start(s32[4]{0:T(128)} %param.21) | copy-start | bytes 52
  119.2 416.6 %all-gather.17.cloned.1.call-start = ((), (), s32[]{:S(2)}) async-start(), calls=%async_computation.6 | async-start | bytes 35651584 | tf_op jit(solution)/shard_map/all_gather | solution.py:132
  119.8 487.3 %reduce-scatter.2.cloned.1.call-start = ((), (), s32[]{:S(2)}) async-start(), calls=%async_computation.7 | async-start | bytes 6291456 | tf_op jit(solution)/shard_map/reduce_scatter | solution.py:135
  309.9 1.6 copy-start.3
  309.9 2.2 copy-start.4
  385.7 15.3 %copy-start.2 = (bf16[4096,256]{1,0:T(8,128)(2,1)S(1)}, bf16[4096,256]{1,0:T(8,128)(2,1)}, u32[]{:S(2)}) copy-start(bf16[4096,256]{1,0:T(8,128)(2,1)} %get-tuple-element.452) | copy-start | bytes 6291460 | tf_op jit(solution)/shard_map/while
  437.3 15.6 %copy-start.2 = (bf16[4096,256]{1,0:T(8,128)(2,1)S(1)}, bf16[4096,256]{1,0:T(8,128)(2,1)}, u32[]{:S(2)}) copy-start(bf16[4096,256]{1,0:T(8,128)(2,1)} %get-tuple-element.452) | copy-start | bytes 6291460 | tf_op jit(solution)/shard_map/while
  552.6 59.3 %copy-start.1 = (bf16[512,512]{1,0:T(8,128)(2,1)S(1)}, bf16[512,512]{1,0:T(8,128)(2,1)}, u32[]{:S(2)}) copy-start(bf16[512,512]{1,0:T(8,128)(2,1)} %param.15) | copy-start | bytes 1572868
Sparse Core Ops, SparseCore 0:
  9.5 53.1 all-gather.6
  64.8 48.8 all-gather.12
  115.4 166.5 all-gather.10
  284.0 41.0 all-gather.8
  327.1 40.5 all-gather.14
  369.1 166.7 all-gather.16
  552.8 54.3 reduce-scatter.1
where the time goes:
time: 619 us
  waiting for transfers between devices  423 us (68%)
  matrix products  109 us (18%)
  other arithmetic  50.7 us (8%)
  local copies, waits for them, and re-layouts  21.9 us (4%)
  between operations  13.7 us (2%)
    all_gather x1, waiting for transfers between devices, shards(): lax.all_gather(w_query, 'fsdp', axis=0, tiled=True)  162 us
    all_gather x1, waiting for transfers between devices, shards(): lax.all_gather(w_out, 'fsdp', axis=1, tiled=True)  59.9 us
    reduce_scatter x1, waiting for transfers between devices, shards(): lax.psum_scatter(terms.astype(jnp.bfloat16), 'tp', scatter_dimension=0, t...  54.5 us
    all_gather x1, waiting for transfers between devices, shards(): lax.all_gather(key_part, 'fsdp', axis=0, tiled=True)  45.9 us
    all_gather x1, waiting for transfers between devices, shards(): lax.all_gather(value_part, 'fsdp', axis=0, tiled=True)  44.6 us
    all_gather x1, waiting for transfers between devices, shards(): value_piece = lax.all_gather(values, 'fsdp', axis=0, tiled=True)  42.6 us
    dot_general x2, matrix products, fold_block(): jnp.einsum('kgqn,nkd->kgqd', weights.astype(jnp.bfloat16), value_block, p...  35.9 us
    reduce_sum x2, other arithmetic, fold_block(): total = total * factor + jnp.sum(weights, axis=3)  30.9 us
  transfers between devices with their start and end apart: 7, of which 7 were waited for; matrix products, arithmetic and copies ran while one was open for 25% of the time, Pallas kernels for 0%

commit v1 on v0

--- a/solution.py
+++ b/solution.py
@@ -78,7 +78,12 @@
         jnp.zeros((local_kv, per_kv, tok_rows, HEAD), jnp.float32),
     )
     key_piece = lax.all_gather(keys, "fsdp", axis=0, tiled=True)
-    value_piece = lax.all_gather(values, "fsdp", axis=0, tiled=True)
+    ring = [values]
+    for hop in range(15):
+        ring.append(lax.ppermute(ring[-1], "fsdp", [(dev, (dev + 1) % 16) for dev in range(16)]))
+    value_piece = jnp.roll(
+        jnp.concatenate(ring[::-1], axis=0), (lax.axis_index("fsdp") + 1) * ring[0].shape[0], axis=0
+    )
     piece_rows = key_piece.shape[0]
     shard_count = max(piece_rows // tok_rows, 1)
     per_block = 1

time: 619 us -> 597 us (0.964)
  waiting for transfers between devices: 423 us -> 399 us
    ppermute x0 -> x15, waiting for transfers between devices: none -> 148 us  [shards(): lax.ppermute(ring[-1], 'fsdp', [(dev, (dev + 1) % 16) for dev in range(16)])]
    all_gather x1, waiting for transfers between devices: 162 us -> 33.6 us  [shards(): lax.all_gather(w_query, 'fsdp', axis=0, tiled=True)]
    all_gather x1 -> x0, waiting for transfers between devices: 42.6 us -> none  [shards(): value_piece = lax.all_gather(values, 'fsdp', axis=0, tiled=True)]
  transfers between devices with their start and end apart: 7 -> 21, of which waited for: 7 -> 21; matrix products, arithmetic and copies ran while one was open for 25% -> 26% of each run, Pallas kernels for 0% -> 0%
where the time goes in v1:
time: 597 us; the launch traced here: 596 us
  waiting for transfers between devices  399 us (67%)
  matrix products  109 us (18%)
  other arithmetic  50.5 us (8%)
  local copies, waits for them, and re-layouts  23.5 us (4%)
  between operations  13.9 us (2%)
    ppermute x15, waiting for transfers between devices, shards(): lax.ppermute(ring[-1], 'fsdp', [(dev, (dev + 1) % 16) for dev in range(16)])  148 us
    all_gather x1, waiting for transfers between devices, shards(): lax.all_gather(w_out, 'fsdp', axis=1, tiled=True)  60.7 us
    reduce_scatter x1, waiting for transfers between devices, shards(): lax.psum_scatter(terms.astype(jnp.bfloat16), 'tp', scatter_dimension=0, t...  54.5 us
    all_gather x1, waiting for transfers between devices, shards(): lax.all_gather(key_part, 'fsdp', axis=0, tiled=True)  45.9 us
    all_gather x1, waiting for transfers between devices, shards(): lax.all_gather(value_part, 'fsdp', axis=0, tiled=True)  44 us
    dot_general x2, matrix products, fold_block(): jnp.einsum('kgqn,nkd->kgqd', weights.astype(jnp.bfloat16), value_block, p...  35.8 us
    all_gather x1, waiting for transfers between devices, shards(): lax.all_gather(w_query, 'fsdp', axis=0, tiled=True)  33.6 us
    reduce_sum x2, other arithmetic, fold_block(): total = total * factor + jnp.sum(weights, axis=3)  30.6 us
  transfers between devices with their start and end apart: 21, of which 21 were waited for; matrix products, arithmetic and copies ran while one was open for 26% of the time, Pallas kernels for 0%

profile of v1, /device:TPU:0, one launch (start us, length us, event | category | flops | bytes accessed | tf_op | source)
XLA Modules:
  0.0 596.3 jit_solution(7130515803802161593)
XLA Ops:
  8.4 1.7 constant_dynamic-slice_fusion.3
  13.6 3.1 fusion.15
  16.7 45.9 %all-gather.6.cloned.1.call-done = bf16[8192,256]{1,0:T(8,128)(2,1)} async-done(((bf16[512,256]{1,0:T(8,128)(2,1)}), bf16[8192,256]{1,0:T(8,128)(2,1)}) %all-gather.6.cloned.1.call-update) | async-done | bytes 4194320 | tf_op jit(solution)/shard_map/all_gather | solution.py:59
  62.6 5.6 convolution_add_fusion.2
  69.7 44.0 %all-gather.12.cloned.1.call-done = bf16[8192,256]{1,0:T(8,128)(2,1)} async-done(((bf16[512,256]{1,0:T(8,128)(2,1)}), bf16[8192,256]{1,0:T(8,128)(2,1)}) %all-gather.12.cloned.1.call-update) | async-done | bytes 4194320 | tf_op jit(solution)/shard_map/all_gather | solution.py:60
  113.7 4.8 fusion.20
  118.8 7.7 %collective-permute-done = bf16[256,256]{1,0:T(8,128)(2,1)S(1)} collective-permute-done((bf16[256,256]{1,0:T(8,128)(2,1)S(1)}, bf16[256,256]{1,0:T(8,128)(2,1)S(1)}, u32[]{:S(2)}, u32[]{:S(2)}) %collective-permute-start) | collective-permute-done | bytes 131104 | tf_op jit(solution)/shard_map/ppermute | solution.py:83
  126.5 10.0 %collective-permute-done.1 = bf16[256,256]{1,0:T(8,128)(2,1)S(1)} collective-permute-done((bf16[256,256]{1,0:T(8,128)(2,1)S(1)}, bf16[256,256]{1,0:T(8,128)(2,1)S(1)}, u32[]{:S(2)}, u32[]{:S(2)}) %collective-permute-start.1) | collective-permute-done | bytes 131104 | tf_op jit(solution)/shard_map/ppermute | solution.py:83
  136.5 10.0 %collective-permute-done.2 = bf16[256,256]{1,0:T(8,128)(2,1)S(1)} collective-permute-done((bf16[256,256]{1,0:T(8,128)(2,1)S(1)}, bf16[256,256]{1,0:T(8,128)(2,1)S(1)}, u32[]{:S(2)}, u32[]{:S(2)}) %collective-permute-start.2) | collective-permute-done | bytes 131104 | tf_op jit(solution)/shard_map/ppermute | solution.py:83
  146.6 10.0 %collective-permute-done.3 = bf16[256,256]{1,0:T(8,128)(2,1)S(1)} collective-permute-done((bf16[256,256]{1,0:T(8,128)(2,1)S(1)}, bf16[256,256]{1,0:T(8,128)(2,1)S(1)}, u32[]{:S(2)}, u32[]{:S(2)}) %collective-permute-start.3) | collective-permute-done | bytes 131104 | tf_op jit(solution)/shard_map/ppermute | solution.py:83
  156.6 10.0 %collective-permute-done.4 = bf16[256,256]{1,0:T(8,128)(2,1)S(1)} collective-permute-done((bf16[256,256]{1,0:T(8,128)(2,1)S(1)}, bf16[256,256]{1,0:T(8,128)(2,1)S(1)}, u32[]{:S(2)}, u32[]{:S(2)}) %collective-permute-start.4) | collective-permute-done | bytes 131104 | tf_op jit(solution)/shard_map/ppermute | solution.py:83
  166.6 10.0 %collective-permute-done.5 = bf16[256,256]{1,0:T(8,128)(2,1)S(1)} collective-permute-done((bf16[256,256]{1,0:T(8,128)(2,1)S(1)}, bf16[256,256]{1,0:T(8,128)(2,1)S(1)}, u32[]{:S(2)}, u32[]{:S(2)}) %collective-permute-start.5) | collective-permute-done | bytes 131104 | tf_op jit(solution)/shard_map/ppermute | solution.py:83
  176.6 10.0 %collective-permute-done.6 = bf16[256,256]{1,0:T(8,128)(2,1)S(1)} collective-permute-done((bf16[256,256]{1,0:T(8,128)(2,1)S(1)}, bf16[256,256]{1,0:T(8,128)(2,1)S(1)}, u32[]{:S(2)}, u32[]{:S(2)}) %collective-permute-start.6) | collective-permute-done | bytes 131104 | tf_op jit(solution)/shard_map/ppermute | solution.py:83
  186.7 10.0 %collective-permute-done.7 = bf16[256,256]{1,0:T(8,128)(2,1)S(1)} collective-permute-done((bf16[256,256]{1,0:T(8,128)(2,1)S(1)}, bf16[256,256]{1,0:T(8,128)(2,1)S(1)}, u32[]{:S(2)}, u32[]{:S(2)}) %collective-permute-start.7) | collective-permute-done | bytes 131104 | tf_op jit(solution)/shard_map/ppermute | solution.py:83
  196.7 10.0 %collective-permute-done.8 = bf16[256,256]{1,0:T(8,128)(2,1)S(1)} collective-permute-done((bf16[256,256]{1,0:T(8,128)(2,1)S(1)}, bf16[256,256]{1,0:T(8,128)(2,1)S(1)}, u32[]{:S(2)}, u32[]{:S(2)}) %collective-permute-start.8) | collective-permute-done | bytes 131104 | tf_op jit(solution)/shard_map/ppermute | solution.py:83
  206.7 10.0 %collective-permute-done.9 = bf16[256,256]{1,0:T(8,128)(2,1)S(1)} collective-permute-done((bf16[256,256]{1,0:T(8,128)(2,1)S(1)}, bf16[256,256]{1,0:T(8,128)(2,1)S(1)}, u32[]{:S(2)}, u32[]{:S(2)}) %collective-permute-start.9) | collective-permute-done | bytes 131104 | tf_op jit(solution)/shard_map/ppermute | solution.py:83
  216.8 10.0 %collective-permute-done.10 = bf16[256,256]{1,0:T(8,128)(2,1)S(1)} collective-permute-done((bf16[256,256]{1,0:T(8,128)(2,1)S(1)}, bf16[256,256]{1,0:T(8,128)(2,1)S(1)}, u32[]{:S(2)}, u32[]{:S(2)}) %collective-permute-start.10) | collective-permute-done | bytes 131104 | tf_op jit(solution)/shard_map/ppermute | solution.py:83
  226.8 10.0 %collective-permute-done.11 = bf16[256,256]{1,0:T(8,128)(2,1)S(1)} collective-permute-done((bf16[256,256]{1,0:T(8,128)(2,1)S(1)}, bf16[256,256]{1,0:T(8,128)(2,1)S(1)}, u32[]{:S(2)}, u32[]{:S(2)}) %collective-permute-start.11) | collective-permute-done | bytes 131104 | tf_op jit(solution)/shard_map/ppermute | solution.py:83
  236.8 10.0 %collective-permute-done.12 = bf16[256,256]{1,0:T(8,128)(2,1)S(1)} collective-permute-done((bf16[256,256]{1,0:T(8,128)(2,1)S(1)}, bf16[256,256]{1,0:T(8,128)(2,1)S(1)}, u32[]{:S(2)}, u32[]{:S(2)}) %collective-permute-start.12) | collective-permute-done | bytes 131104 | tf_op jit(solution)/shard_map/ppermute | solution.py:83
  246.8 10.0 %collective-permute-done.13 = bf16[256,256]{1,0:T(8,128)(2,1)S(1)} collective-permute-done((bf16[256,256]{1,0:T(8,128)(2,1)S(1)}, bf16[256,256]{1,0:T(8,128)(2,1)S(1)}, u32[]{:S(2)}, u32[]{:S(2)}) %collective-permute-start.13) | collective-permute-done | bytes 131104 | tf_op jit(solution)/shard_map/ppermute | solution.py:83
  257.1 9.8 %collective-permute-done.14 = bf16[256,256]{1,0:T(8,128)(2,1)S(1)} collective-permute-done((bf16[256,256]{1,0:T(8,128)(2,1)S(1)}, bf16[256,256]{1,0:T(8,128)(2,1)S(1)}, u32[]{:S(2)}, u32[]{:S(2)}) %collective-permute-start.14) | collective-permute-done | bytes 131104 | tf_op jit(solution)/shard_map/ppermute | solution.py:83
  267.5 1.5 constant_dynamic-slice_fusion.2
  269.0 33.6 %all-gather.10.cloned.1.call-done = bf16[8192,2048]{1,0:T(8,128)(2,1)} async-done(((bf16[512,2048]{1,0:T(8,128)(2,1)}), bf16[8192,2048]{1,0:T(8,128)(2,1)}) %all-gather.10.cloned.1.call-update) | async-done | bytes 33554448 | tf_op jit(solution)/shard_map/all_gather | solution.py:58
  302.6 16.5 %convolution_add_fusion = f32[256,2048]{1,0:T(8,128)S(1)} fusion(bf16[8192,2048]{1,0:T(8,128)(2,1)} %all-gather.10.cloned.1.call-done, f32[2048]{0:T(1024)S(1)} %convert_element_type.80, bf16[256,8192]{1,0:T(8,128)(2,1)} %param.12, f32[8192]{0:T(1024)S(1)} %copy-done.8, f32[256]{0:T(256)S(1)} %add_rsqrt_fusion), kind=kOutput, calls=%fused_computation.30 | convolution fusion | flops 8598847488 | bytes 39887872 | tf_op jit(solution)/shard_map/dot_general | solution.py:63
  319.1 1.8 copy.44
  320.9 3.1 slice_negate_fusion
  324.0 3.2 copy.45
  327.2 3.1 copy.46
  333.6 11.2 %all-gather.8.cloned.1.call-done = bf16[4096,256]{0,1:T(8,128)(2,1)} async-done(((bf16[256,256]{0,1:T(8,128)(2,1)}), bf16[4096,256]{0,1:T(8,128)(2,1)}) %all-gather.8.cloned.1.call-update) | async-done | bytes 2097168 | tf_op jit(solution)/shard_map/all_gather | solution.py:80
  344.8 104.7 %while.20 = (s32[]{:T(128)}, f32[2,8,256]{2,1,0:T(8,128)S(1)}, f32[2,8,256]{2,1,0:T(8,128)S(1)}, f32[2,8,256,128]{3,2,1,0:T(8,128)}, s32[256]{0:T(256)S(1)}, /*i...) while((s32[]{:T(128)}, f32[2,8,256]{2,1,0:T(8,128)S(1)}, ...), condition=%wide.region_9.10_spmd.clone, body=%wide.region_5.9_spmd.clone.sunk | while | flops 4407209984 | bytes 125086968 | solution.py:128
  344.8 1.3 constant_dynamic-slice_fusion.7
  346.2 1.4 compare_and_fusion.2
  347.7 15.2 %fusion.45 = (f32[2,8,256]{2,1,0:T(8,128)S(1)}, f32[2,2048,256,8]{2,1,3,0:T(8,128)}) fusion(pred[256,2048]{0,1:T(8,128)(4,1)S(1)} %compare_and_fusion.2, bf16[2048,2,128,1]{0,2,3,1:T(8,128)(2,1)S(1)} %bitcast.72, bf16[256,2,8,128]{3,0,2,1:T(8,128)(2,1)S(1)} %get-tuple-element.451), kind=kOutput, calls=%fused_computation.3.clone.1 | convolution fusion | flops 2172645376 | bytes 36192256 | tf_op jit(solution)/shard_map/while/body/eval_jaxpr/qkgd,nkd->kgqn/dot_general | solution.py:107
  362.9 15.3 %fusion.46 = f32[2,8,256]{2,1,0:T(8,128)S(1)} fusion(f32[2,2048,256,8]{2,1,3,0:T(8,128)} %get-tuple-element.413, f32[2,8,256]{2,1,0:T(8,128)S(1)} %select_maximum_fusion.2, pred[256,2048]{0,1:T(8,128)(4,1)S(1)} %compare_and_fusion.2), kind=kLoop, calls=%fused_computation.5.clone.1 | loop fusion | flops 41938944 | bytes 34111488 | tf_op jit(solution)/shard_map/while/body/eval_jaxpr/reduce_sum | solution.py:118
  378.3 1.4 copy.62
  379.7 17.6 %fusion.48 = f32[2,8,256,128]{3,2,1,0:T(8,128)} fusion(f32[2,8,256,128]{3,2,1,0:T(8,128)} %get-tuple-element.433, bf16[2048,2,128,1]{0,2,3,1:T(8,128)(2,1)} %bitcast.73, f32[2,2048,256,8]{2,1,3,0:T(8,128)} %get-tuple-element.413, f32[2,8,256]{2,1,0:T(8,128)S(1)} %select_maximum_fusion.2, pred[256,2048]{0,1:T(8,128)(4,1)S(1)} %compare_and_fusion.2, ...), kind=kOutput, calls=%fused_computation.9.clone.1 | convolution fusion | flops 2190999552 | bytes 39354368 | tf_op jit(solution)/shard_map/while/body/eval_jaxpr/kgqn,nkd->kgqd/dot_general | solution.py:119
  397.3 1.3 constant_dynamic-slice_fusion.7
  398.8 1.4 compare_and_fusion.2
  400.2 14.1 %fusion.45 = (f32[2,8,256]{2,1,0:T(8,128)S(1)}, f32[2,2048,256,8]{2,1,3,0:T(8,128)}) fusion(pred[256,2048]{0,1:T(8,128)(4,1)S(1)} %compare_and_fusion.2, bf16[2048,2,128,1]{0,2,3,1:T(8,128)(2,1)S(1)} %bitcast.72, bf16[256,2,8,128]{3,0,2,1:T(8,128)(2,1)S(1)} %get-tuple-element.451), kind=kOutput, calls=%fused_computation.3.clone.1 | convolution fusion | flops 2172645376 | bytes 36192256 | tf_op jit(solution)/shard_map/while/body/eval_jaxpr/qkgd,nkd->kgqn/dot_general | solution.py:107
  414.4 15.3 %fusion.46 = f32[2,8,256]{2,1,0:T(8,128)S(1)} fusion(f32[2,2048,256,8]{2,1,3,0:T(8,128)} %get-tuple-element.413, f32[2,8,256]{2,1,0:T(8,128)S(1)} %select_maximum_fusion.2, pred[256,2048]{0,1:T(8,128)(4,1)S(1)} %compare_and_fusion.2), kind=kLoop, calls=%fused_computation.5.clone.1 | loop fusion | flops 41938944 | bytes 34111488 | tf_op jit(solution)/shard_map/while/body/eval_jaxpr/reduce_sum | solution.py:118
  429.8 1.4 copy.62
  431.3 18.2 %fusion.48 = f32[2,8,256,128]{3,2,1,0:T(8,128)} fusion(f32[2,8,256,128]{3,2,1,0:T(8,128)} %get-tuple-element.433, bf16[2048,2,128,1]{0,2,3,1:T(8,128)(2,1)} %bitcast.73, f32[2,2048,256,8]{2,1,3,0:T(8,128)} %get-tuple-element.413, f32[2,8,256]{2,1,0:T(8,128)S(1)} %select_maximum_fusion.2, pred[256,2048]{0,1:T(8,128)(4,1)S(1)} %compare_and_fusion.2, ...), kind=kOutput, calls=%fused_computation.9.clone.1 | convolution fusion | flops 2190999552 | bytes 39354368 | tf_op jit(solution)/shard_map/while/body/eval_jaxpr/kgqn,nkd->kgqd/dot_general | solution.py:119
  449.5 1.9 copy.48
  451.4 1.2 divide_convert_fusion
  452.6 60.7 %all-gather.14.cloned.1.call-done = bf16[2048,8192]{1,0:T(8,128)(2,1)} async-done(((bf16[2048,512]{1,0:T(8,128)(2,1)}), bf16[2048,8192]{1,0:T(8,128)(2,1)}) %all-gather.14.cloned.1.call-update) | async-done | bytes 33554448 | tf_op jit(solution)/shard_map/all_gather | solution.py:137
  513.3 16.8 %convolution_convert_fusion = bf16[256,8192]{1,0:T(8,128)(2,1)} fusion(bf16[256,2048]{0,1:T(8,128)(2,1)} %bitcast.77, bf16[2048,8192]{1,0:T(8,128)(2,1)} %all-gather.14.cloned.1.call-done), kind=kOutput, calls=%fused_computation.25 | convolution fusion | flops 8592031744 | bytes 38797312 | tf_op jit(solution)/shard_map/dot_general | solution.py:135
  530.1 54.5 %reduce-scatter.2.cloned.1.call-done = bf16[128,8192]{1,0:T(8,128)(2,1)} async-done(((bf16[256,8192]{1,0:T(8,128)(2,1)}), bf16[128,8192]{1,0:T(8,128)(2,1)}) %reduce-scatter.2.cloned.1.call-update) | async-done | bytes 2097168 | tf_op jit(solution)/shard_map/reduce_scatter | solution.py:140
  584.7 4.8 convert_add_fusion
  (121 shorter events, 11.3 us)
Async XLA Ops:
  6.5 1.0 copy-start
  6.5 7.0 %copy-start.6 = (bf16[512]{0:T(512)(128)(2,1)S(1)}, bf16[512]{0:T(512)(128)(2,1)}, u32[]{:S(2)}) copy-start(bf16[512]{0:T(512)(128)(2,1)} %param.18) | copy-start | bytes 3076
  6.5 56.1 %all-gather.6.cloned.1.call-start = ((), (), s32[]{:S(2)}) async-start(), calls=%async_computation.1 | async-start | bytes 4456448 | tf_op jit(solution)/shard_map/all_gather | solution.py:59
  8.3 54.3 %copy-start.8 = (f32[8192]{0:T(1024)S(1)}, f32[8192]{0:T(1024)}, u32[]{:S(2)}) copy-start(f32[8192]{0:T(1024)} %param.13) | copy-start | bytes 98308
  8.3 105.4 %all-gather.12.cloned.1.call-start = ((), (), s32[]{:S(2)}) async-start(), calls=%async_computation.4 | async-start | bytes 4456448 | tf_op jit(solution)/shard_map/all_gather | solution.py:60
  10.1 292.5 %all-gather.10.cloned.1.call-start = ((), (), s32[]{:S(2)}) async-start(), calls=%async_computation.3 | async-start | bytes 35651584 | tf_op jit(solution)/shard_map/all_gather | solution.py:58
  10.8 334.0 %all-gather.8.cloned.1.call-start = ((), (), s32[]{:S(2)}) async-start(), calls=%async_computation.2 | async-start | bytes 2228224 | tf_op jit(solution)/shard_map/all_gather | solution.py:80
  68.2 1.4 copy-start.7
  69.0 444.3 %all-gather.14.cloned.1.call-start = ((), (), s32[]{:S(2)}) async-start(), calls=%async_computation.5 | async-start | bytes 35651584 | tf_op jit(solution)/shard_map/all_gather | solution.py:137
  69.6 515.1 %reduce-scatter.2.cloned.1.call-start = ((), (), s32[]{:S(2)}) async-start(), calls=%async_computation.6 | async-start | bytes 6291456 | tf_op jit(solution)/shard_map/reduce_scatter | solution.py:140
  69.7 187.1 %copy-start.5 = (bf16[2048]{0:T(1024)(128)(2,1)S(1)}, bf16[2048]{0:T(1024)(128)(2,1)}, u32[]{:S(2)}) copy-start(bf16[2048]{0:T(1024)(128)(2,1)} %param.17) | copy-start | bytes 12292
  69.7 187.2 %copy-start.9 = (s32[4]{0:T(128)S(1)}, s32[4]{0:T(128)}, u32[]{:S(2)}) copy-start(s32[4]{0:T(128)} %param.21) | copy-start | bytes 52
  118.5 8.0 %collective-permute-start = (bf16[256,256]{1,0:T(8,128)(2,1)S(1)}, bf16[256,256]{1,0:T(8,128)(2,1)S(1)}, u32[]{:S(2)}, u32[]{:S(2)}) collective-permute-start(bf16[256,256]{1,0:T(8,128)(2,1)S(1)} %fusion.20), channel_id=1, source_target_pairs={{0,2},{2,4},{4,6},{6,8},{8,10},{10,12},{12,14},{14,16},{16,18},{18... | collective-permute-start | bytes 393224 | tf_op jit(solution)/shard_map/ppermute | solution.py:83
  126.5 10.0 %collective-permute-start.1 = (bf16[256,256]{1,0:T(8,128)(2,1)S(1)}, bf16[256,256]{1,0:T(8,128)(2,1)S(1)}, u32[]{:S(2)}, u32[]{:S(2)}) collective-permute-start(bf16[256,256]{1,0:T(8,128)(2,1)S(1)} %collective-permute-done), channel_id=1, source_target_pairs={{0,2},{2,4},{4,6},{6,8},{8,10},{10,12},{12,14},{14,16},{16,18},{18... | collective-permute-start | bytes 393224 | tf_op jit(solution)/shard_map/ppermute | solution.py:83
  136.5 10.0 %collective-permute-start.2 = (bf16[256,256]{1,0:T(8,128)(2,1)S(1)}, bf16[256,256]{1,0:T(8,128)(2,1)S(1)}, u32[]{:S(2)}, u32[]{:S(2)}) collective-permute-start(bf16[256,256]{1,0:T(8,128)(2,1)S(1)} %collective-permute-done.1), channel_id=1, source_target_pairs={{0,2},{2,4},{4,6},{6,8},{8,10},{10,12},{12,14},{14,16},{16,18},{18... | collective-permute-start | bytes 393224 | tf_op jit(solution)/shard_map/ppermute | solution.py:83
  146.5 10.0 %collective-permute-start.3 = (bf16[256,256]{1,0:T(8,128)(2,1)S(1)}, bf16[256,256]{1,0:T(8,128)(2,1)S(1)}, u32[]{:S(2)}, u32[]{:S(2)}) collective-permute-start(bf16[256,256]{1,0:T(8,128)(2,1)S(1)} %collective-permute-done.2), channel_id=1, source_target_pairs={{0,2},{2,4},{4,6},{6,8},{8,10},{10,12},{12,14},{14,16},{16,18},{18... | collective-permute-start | bytes 393224 | tf_op jit(solution)/shard_map/ppermute | solution.py:83
  156.6 10.0 %collective-permute-start.4 = (bf16[256,256]{1,0:T(8,128)(2,1)S(1)}, bf16[256,256]{1,0:T(8,128)(2,1)S(1)}, u32[]{:S(2)}, u32[]{:S(2)}) collective-permute-start(bf16[256,256]{1,0:T(8,128)(2,1)S(1)} %collective-permute-done.3), channel_id=1, source_target_pairs={{0,2},{2,4},{4,6},{6,8},{8,10},{10,12},{12,14},{14,16},{16,18},{18... | collective-permute-start | bytes 393224 | tf_op jit(solution)/shard_map/ppermute | solution.py:83
  166.6 10.0 %collective-permute-start.5 = (bf16[256,256]{1,0:T(8,128)(2,1)S(1)}, bf16[256,256]{1,0:T(8,128)(2,1)S(1)}, u32[]{:S(2)}, u32[]{:S(2)}) collective-permute-start(bf16[256,256]{1,0:T(8,128)(2,1)S(1)} %collective-permute-done.4), channel_id=1, source_target_pairs={{0,2},{2,4},{4,6},{6,8},{8,10},{10,12},{12,14},{14,16},{16,18},{18... | collective-permute-start | bytes 393224 | tf_op jit(solution)/shard_map/ppermute | solution.py:83
  176.6 10.0 %collective-permute-start.6 = (bf16[256,256]{1,0:T(8,128)(2,1)S(1)}, bf16[256,256]{1,0:T(8,128)(2,1)S(1)}, u32[]{:S(2)}, u32[]{:S(2)}) collective-permute-start(bf16[256,256]{1,0:T(8,128)(2,1)S(1)} %collective-permute-done.5), channel_id=1, source_target_pairs={{0,2},{2,4},{4,6},{6,8},{8,10},{10,12},{12,14},{14,16},{16,18},{18... | collective-permute-start | bytes 393224 | tf_op jit(solution)/shard_map/ppermute | solution.py:83
  186.7 10.0 %collective-permute-start.7 = (bf16[256,256]{1,0:T(8,128)(2,1)S(1)}, bf16[256,256]{1,0:T(8,128)(2,1)S(1)}, u32[]{:S(2)}, u32[]{:S(2)}) collective-permute-start(bf16[256,256]{1,0:T(8,128)(2,1)S(1)} %collective-permute-done.6), channel_id=1, source_target_pairs={{0,2},{2,4},{4,6},{6,8},{8,10},{10,12},{12,14},{14,16},{16,18},{18... | collective-permute-start | bytes 393224 | tf_op jit(solution)/shard_map/ppermute | solution.py:83
  196.7 10.0 %collective-permute-start.8 = (bf16[256,256]{1,0:T(8,128)(2,1)S(1)}, bf16[256,256]{1,0:T(8,128)(2,1)S(1)}, u32[]{:S(2)}, u32[]{:S(2)}) collective-permute-start(bf16[256,256]{1,0:T(8,128)(2,1)S(1)} %collective-permute-done.7), channel_id=1, source_target_pairs={{0,2},{2,4},{4,6},{6,8},{8,10},{10,12},{12,14},{14,16},{16,18},{18... | collective-permute-start | bytes 393224 | tf_op jit(solution)/shard_map/ppermute | solution.py:83
  206.7 10.0 %collective-permute-start.9 = (bf16[256,256]{1,0:T(8,128)(2,1)S(1)}, bf16[256,256]{1,0:T(8,128)(2,1)S(1)}, u32[]{:S(2)}, u32[]{:S(2)}) collective-permute-start(bf16[256,256]{1,0:T(8,128)(2,1)S(1)} %collective-permute-done.8), channel_id=1, source_target_pairs={{0,2},{2,4},{4,6},{6,8},{8,10},{10,12},{12,14},{14,16},{16,18},{18... | collective-permute-start | bytes 393224 | tf_op jit(solution)/shard_map/ppermute | solution.py:83
  216.7 10.0 %collective-permute-start.10 = (bf16[256,256]{1,0:T(8,128)(2,1)S(1)}, bf16[256,256]{1,0:T(8,128)(2,1)S(1)}, u32[]{:S(2)}, u32[]{:S(2)}) collective-permute-start(bf16[256,256]{1,0:T(8,128)(2,1)S(1)} %collective-permute-done.9), channel_id=1, source_target_pairs={{0,2},{2,4},{4,6},{6,8},{8,10},{10,12},{12,14},{14,16},{16,18},{18... | collective-permute-start | bytes 393224 | tf_op jit(solution)/shard_map/ppermute | solution.py:83
  226.8 10.0 %collective-permute-start.11 = (bf16[256,256]{1,0:T(8,128)(2,1)S(1)}, bf16[256,256]{1,0:T(8,128)(2,1)S(1)}, u32[]{:S(2)}, u32[]{:S(2)}) collective-permute-start(bf16[256,256]{1,0:T(8,128)(2,1)S(1)} %collective-permute-done.10), channel_id=1, source_target_pairs={{0,2},{2,4},{4,6},{6,8},{8,10},{10,12},{12,14},{14,16},{16,18},{18... | collective-permute-start | bytes 393224 | tf_op jit(solution)/shard_map/ppermute | solution.py:83
  236.8 10.0 %collective-permute-start.12 = (bf16[256,256]{1,0:T(8,128)(2,1)S(1)}, bf16[256,256]{1,0:T(8,128)(2,1)S(1)}, u32[]{:S(2)}, u32[]{:S(2)}) collective-permute-start(bf16[256,256]{1,0:T(8,128)(2,1)S(1)} %collective-permute-done.11), channel_id=1, source_target_pairs={{0,2},{2,4},{4,6},{6,8},{8,10},{10,12},{12,14},{14,16},{16,18},{18... | collective-permute-start | bytes 393224 | tf_op jit(solution)/shard_map/ppermute | solution.py:83
  246.8 10.0 %collective-permute-start.13 = (bf16[256,256]{1,0:T(8,128)(2,1)S(1)}, bf16[256,256]{1,0:T(8,128)(2,1)S(1)}, u32[]{:S(2)}, u32[]{:S(2)}) collective-permute-start(bf16[256,256]{1,0:T(8,128)(2,1)S(1)} %collective-permute-done.12), channel_id=1, source_target_pairs={{0,2},{2,4},{4,6},{6,8},{8,10},{10,12},{12,14},{14,16},{16,18},{18... | collective-permute-start | bytes 393224 | tf_op jit(solution)/shard_map/ppermute | solution.py:83
  256.9 10.0 %collective-permute-start.14 = (bf16[256,256]{1,0:T(8,128)(2,1)S(1)}, bf16[256,256]{1,0:T(8,128)(2,1)S(1)}, u32[]{:S(2)}, u32[]{:S(2)}) collective-permute-start(bf16[256,256]{1,0:T(8,128)(2,1)S(1)} %collective-permute-done.13), channel_id=1, source_target_pairs={{0,2},{2,4},{4,6},{6,8},{8,10},{10,12},{12,14},{14,16},{16,18},{18... | collective-permute-start | bytes 393224 | tf_op jit(solution)/shard_map/ppermute | solution.py:83
  330.4 1.6 copy-start.3
  330.4 2.2 copy-start.4
  362.9 15.3 %copy-start.2 = (bf16[4096,256]{1,0:T(8,128)(2,1)S(1)}, bf16[4096,256]{1,0:T(8,128)(2,1)}, u32[]{:S(2)}) copy-start(bf16[4096,256]{1,0:T(8,128)(2,1)} %get-tuple-element.452) | copy-start | bytes 6291460 | tf_op jit(solution)/shard_map/while
  414.4 15.4 %copy-start.2 = (bf16[4096,256]{1,0:T(8,128)(2,1)S(1)}, bf16[4096,256]{1,0:T(8,128)(2,1)}, u32[]{:S(2)}) copy-start(bf16[4096,256]{1,0:T(8,128)(2,1)} %get-tuple-element.452) | copy-start | bytes 6291460 | tf_op jit(solution)/shard_map/while
  530.1 59.3 %copy-start.1 = (bf16[512,512]{1,0:T(8,128)(2,1)S(1)}, bf16[512,512]{1,0:T(8,128)(2,1)}, u32[]{:S(2)}) copy-start(bf16[512,512]{1,0:T(8,128)(2,1)} %param.15) | copy-start | bytes 1572868
Sparse Core Ops, SparseCore 0:
  9.5 53.0 all-gather.5
  64.8 48.8 all-gather.11
  115.3 187.2 all-gather.9
  304.6 40.1 all-gather.7
  346.2 167.1 all-gather.13
  530.2 54.3 reduce-scatter.1
